TPU v7x, 32 devices: a whole 2x2x4 slice. The times are simulated.
32 devices in a mesh: ctx: 16 (over z, y, core), head: 2 (over x).
Axes of the slice: x: 2, y: 2, z: 4, core: 2. Of those that a mesh axis runs over, the one named last changes fastest.
Arguments:
- queries: bfloat16 [8192, 16, 128], P('ctx', 'head'), may hold values from -130 to 130, as said below
- values: bfloat16 [8192, 16, 128], P('ctx', 'head'), may hold values from -6 to 6
- codes: int32 [8192, 16], P('ctx', 'head'), may hold values from 0 to 511
- codebook: bfloat16 [16, 512, 128], P('head'), may hold values from -8 to 8, as said below
- out_weight: bfloat16 [2048, 2048], P('head'), may hold values from -0.1875 to 0.1875
Outputs:
- mixed: bfloat16 [8192, 2048], P('ctx', 'head')
Inputs may be any that keep to these rules, and one draw needn't show every extreme that they name: `queries`: every entry has magnitude at most 130. `codebook`: every entry has magnitude at most 8.
All inputs are finite; a program needn't handle non-finite values.
Results may differ from a plain program's by a relative error of at most 0.0066.
Values may be sent and summed in bfloat16 or wider, within the bound.
No kernel may reach another device: no remote copies, remote signals or barrier semaphores. Data moves between devices by JAX's collectives and lax.ppermute only.
A program may use at most 128 MiB of HBM per device.

v0:
```python
import jax
import jax.numpy as jnp
from jax import lax
from jax.sharding import PartitionSpec as P

BLOCK = 512


def from_behind(value, axis, steps):
    count = lax.axis_size(axis)
    first, last = (max(0, -steps), min(count, count - steps))
    return lax.ppermute(value, axis, [(source, source + steps) for source in range(first, last)])


def prefix(x, axis, combine, identity):
    devices, here = (lax.axis_size(axis), lax.axis_index(axis))
    everything = jax.tree.map(lambda part: lax.all_gather(part, axis), x)
    start = jax.tree.map(
        lambda part, zero: jnp.broadcast_to(jnp.asarray(zero, part.dtype), part.shape), x, identity
    )

    def turn(k, before):
        reached = k < here
        new = combine(before, jax.tree.map(lambda part: part[k], everything))
        return jax.tree.map(lambda a, b: jnp.where(reached, a, b), new, before)

    return lax.fori_loop(0, devices, turn, start)


def attend(query, cur_keys, cur_values, prev_keys, prev_values, live, book, cache_sum, cache_count):
    scale = query.shape[-1] ** (-0.5)
    code_scores = jnp.dot(query, book.T, preferred_element_type=jnp.float32) * scale
    cur_scores = jnp.dot(query, cur_keys.T, preferred_element_type=jnp.float32) * scale
    prev_scores = jnp.dot(query, prev_keys.T, preferred_element_type=jnp.float32) * scale
    rows = lax.broadcasted_iota(jnp.int32, cur_scores.shape, 0)
    cols = lax.broadcasted_iota(jnp.int32, cur_scores.shape, 1)
    causal = rows >= cols
    present = (cache_count > 0.0)[None, :]
    top = jnp.max(jnp.where(causal, cur_scores, -jnp.inf), axis=1)
    top = jnp.maximum(top, jnp.max(jnp.where(live, prev_scores, -jnp.inf), axis=1))
    top = jnp.maximum(top, jnp.max(jnp.where(present, code_scores, -jnp.inf), axis=1))
    top = top[:, None]
    cur_weight = jnp.where(causal, jnp.exp(cur_scores - top), 0.0)
    prev_weight = jnp.where(live, jnp.exp(prev_scores - top), 0.0)
    code_weight = jnp.where(present, jnp.exp(code_scores - top), 0.0)
    denom = (
        jnp.sum(cur_weight, axis=1)
        + jnp.sum(prev_weight, axis=1)
        + jnp.sum(code_weight * cache_count[None, :], axis=1)
    )
    numer = jnp.dot(cur_weight.astype(jnp.bfloat16), cur_values, preferred_element_type=jnp.float32)
    numer = numer + jnp.dot(
        prev_weight.astype(jnp.bfloat16), prev_values, preferred_element_type=jnp.float32
    )
    numer = numer + jnp.dot(code_weight, cache_sum, precision=lax.Precision.HIGHEST)
    return (numer / denom[:, None]).astype(jnp.bfloat16)


def add_totals(earlier, later):
    return (earlier[0] + later[0], earlier[1] + later[1])


def on_device(queries, values, codes, codebook, out_weight):
    tokens, local_heads, width = queries.shape
    ncodes = codebook.shape[1]
    nblocks = tokens // BLOCK
    keys = jax.vmap(lambda book, index: book[index], in_axes=(0, 1), out_axes=1)(codebook, codes)
    table = lax.broadcasted_iota(jnp.int32, (1, 1, ncodes), 2)
    onehot = (
        (codes[:, :, None] == table)
        .astype(jnp.bfloat16)
        .reshape(nblocks, BLOCK, local_heads, ncodes)
    )
    block_sums = jnp.einsum(
        "bths,bthd->bhsd",
        onehot,
        values.reshape(nblocks, BLOCK, local_heads, width),
        preferred_element_type=jnp.float32,
    )
    block_counts = jnp.sum(onehot.astype(jnp.float32), axis=1)
    last_sum, last_count = (block_sums[nblocks - 1], block_counts[nblocks - 1])
    rest_sum = jnp.sum(block_sums[: nblocks - 1], axis=0)
    rest_count = jnp.sum(block_counts[: nblocks - 1], axis=0)
    prev_keys, prev_values = from_behind((keys, values), "ctx", 1)
    zero_sum = jnp.zeros_like(last_sum)
    zero_count = jnp.zeros_like(last_count)
    total_sum, total_count = prefix(
        (rest_sum + last_sum, rest_count + last_count), "ctx", add_totals, (zero_sum, zero_count)
    )
    pend_sum, pend_count = from_behind((last_sum, last_count), "ctx", 1)
    cache_sum = total_sum - pend_sum
    cache_count = total_count - pend_count
    live = lax.axis_index("ctx") > 0
    attended = jax.vmap(attend, in_axes=(1, 1, 1, 1, 1, None, 0, 0, 0), out_axes=1)(
        queries, keys, values, prev_keys, prev_values, live, codebook, cache_sum, cache_count
    )
    attended_all = attended.reshape(tokens, local_heads * width)
    columns = lax.all_to_all(out_weight, "head", split_axis=1, concat_axis=0, tiled=True)
    summed = jnp.dot(
        lax.all_gather(attended_all, "head", axis=1, tiled=True),
        columns,
        preferred_element_type=jnp.float32,
    )
    return summed.astype(jnp.bfloat16)


def solution(mesh):
    return jax.shard_map(
        on_device,
        mesh=mesh,
        in_specs=(
            P("ctx", "head", None),
            P("ctx", "head", None),
            P("ctx", "head"),
            P("head", None, None),
            P("head", None),
        ),
        out_specs=P("ctx", "head"),
        check_vma=False,
    )
```

profile of v0, /device:TPU:0, one launch (start us, length us, event | category | flops | bytes accessed | tf_op | source)
XLA Modules:
  0.0 355.7 jit_solution(16759261698368009623)
XLA Ops:
  6.5 2.5 copy.66
  9.0 4.0 %fusion.3 = f32[8,512,128]{2,1,0:T(8,128)} fusion(bf16[512,8,128]{0,2,1:T(8,128)(2,1)} %copy.66, s32[512,8]{0,1:T(8,128)} %param.9), kind=kOutput, calls=%fused_computation.18 | convolution fusion | flops 538968064 | bytes 3162112 | tf_op jit(solution)/shard_map/bths,bthd->bhsd/dot_general | solution.py:74
  13.0 0.0 all-gather.7.cloned.1.call-update
  13.1 40.2 %gather_fusion = bf16[4096,128]{1,0:T(8,128)(2,1)} fusion(bf16[8,512,128]{2,1,0:T(8,128)(2,1)S(1)} %copy-done, s32[4096]{0:T(1024)S(1)} %bitcast.65), kind=kCustom, calls=%fused_computation | custom fusion | bytes 2129920 | tf_op jit(solution)/shard_map/vmap()/gather | solution.py:67
  53.3 3.4 collective-permute-start
  56.6 4.5 %collective-permute-start.2 = (bf16[512,8,128]{0,2,1:T(8,128)(2,1)}, bf16[512,8,128]{0,2,1:T(8,128)(2,1)}, u32[]{:S(2)}, u32[]{:S(2)}) collective-permute-start(bf16[512,8,128]{0,2,1:T(8,128)(2,1)} %copy.66), channel_id=1, source_target_pairs={{0,2},{2,4},{4,6},{6,8},{8,10},{10,12},{12,14},{14,16},{16,18},{18... | collective-permute-start | bytes 3145736 | tf_op jit(solution)/shard_map/ppermute | solution.py:12
  61.2 2.6 collective-permute-start.3
  63.8 0.1 copy.63
  63.9 1.0 convert_reduce_fusion
  64.9 1.9 collective-permute-start.1
  66.8 6.5 %copy.70 = bf16[1024,2048]{0,1:T(8,128)(2,1)} copy(bf16[1024,2048]{1,0:T(8,128)(2,1)} %param.11) | data formatting | bytes 8388608 | tf_op args[4]
  73.2 5.6 %all-to-all-start = ((bf16[1024,2,1024]{0,2,1:T(8,128)(2,1)}), bf16[1024,2,1024]{0,2,1:T(8,128)(2,1)}, u32[]{:S(2)}, u32[]{:S(2)}) async-start(bf16[1024,2,1024]{0,2,1:T(8,128)(2,1)} %bitcast.70), calls=%async_computation | async-start | bytes 8388608 | tf_op jit(solution)/shard_map/all_to_all | solution.py:98
  78.8 0.0 all-gather.5.cloned.1.call-start
  78.9 0.0 copy-start.2
  78.9 0.1 iota_compare_fusion.3
  79.0 132.5 %all-gather.1 = f32[128,512]{1,0:T(8,128)} all-gather(f32[8,512]{1,0:T(8,128)S(1)} %convert_reduce_fusion), channel_id=3, replica_groups=mesh['ctx'=16,'head'=2] {'ctx'}, dimensions={0}, use_global_device_ids=true | all-gather | bytes 278528 | tf_op jit(solution)/shard_map/all_gather | solution.py:17
  211.5 6.2 %fusion = (f32[8,512]{1,0:T(8,128)S(1)}, f32[8,512,512]{2,1,0:T(8,128)}) fusion(pred[512,512]{0,1:T(8,128)(4,1)S(1)} %iota_compare_fusion.3, bf16[8,512,128]{2,1,0:T(8,128)(2,1)} %bitcast.2, bf16[512,8,128]{2,1,0:T(8,128)(2,1)} %param.7), kind=kOutput, calls=%fused_computation.7 | convolution fusion | flops 543158272 | bytes 10764288 | tf_op jit(solution)/shard_map/vmap()/dot_general | solution.py:33
  217.7 0.0 collective-permute-done
  217.7 5.7 %select_reduce_fusion.1 = (f32[8,512]{1,0:T(8,128)S(1)}, f32[8,512,512]{1,2,0:T(8,128)}) fusion(pred[]{:T(512)S(6)} %gt.6, bf16[512,8,128]{2,1,0:T(8,128)(2,1)S(1)} %copy-done.2, bf16[512,8,128]{2,0,1:T(8,128)(2,1)} %collective-permute-done), kind=kOutput, calls=%fused_computation.17 | convolution fusion | flops 543158272 | bytes 10502145 | tf_op jit(solution)/shard_map/vmap()/dot_general | solution.py:34
  223.4 3.9 %all-gather.7.cloned.1.call-done = f32[128,512,128]{2,1,0:T(8,128)} async-done(((f32[8,512,128]{2,1,0:T(8,128)}), f32[128,512,128]{2,1,0:T(8,128)}) %all-gather.7.cloned.1.call-update) | async-done | bytes 33554448 | tf_op jit(solution)/shard_map/all_gather | solution.py:17
  227.3 48.6 %while.16 = (s32[]{:T(128)}, f32[8,512,128]{2,1,0:T(8,128)S(1)}, f32[8,512]{1,0:T(8,128)S(1)}, s32[]{:T(128)}, f32[16,8,512,128]{3,2,1,0:T(8,128)}, /*index=5*/f32[16,8,512]{2,1,0:T(8,128)}, s32[]{:T(128)}, s32[]{:T(128)}) while((s32[]{:T(128)}, f32[8,512,128]{2,1,0:T(8,128)S(1)}, f32[8,512]{1,0:T(8,128)S(1)}, s32[]{:T(128)}, ...), condition=%wide.region_4.5_spmd.clone, body=%wide.region_3.4_spmd.clone.sunk | while | flops 1585156 | bytes 6340723 | solution.py:27
  227.3 2.3 add_select_fusion.4
  229.6 0.7 add_select_fusion.5
  230.4 2.3 add_select_fusion.4
  232.7 0.7 add_select_fusion.5
  233.4 2.3 add_select_fusion.4
  235.7 0.7 add_select_fusion.5
  236.4 2.3 add_select_fusion.4
  238.8 0.7 add_select_fusion.5
  239.5 2.3 add_select_fusion.4
  241.8 0.7 add_select_fusion.5
  242.5 2.3 add_select_fusion.4
  244.8 0.7 add_select_fusion.5
  245.5 2.3 add_select_fusion.4
  247.9 0.7 add_select_fusion.5
  248.6 2.3 add_select_fusion.4
  250.9 0.7 add_select_fusion.5
  251.6 2.3 add_select_fusion.4
  253.9 0.7 add_select_fusion.5
  254.7 2.3 add_select_fusion.4
  257.0 0.7 add_select_fusion.5
  257.7 2.3 add_select_fusion.4
  260.0 0.7 add_select_fusion.5
  260.7 2.3 add_select_fusion.4
  263.0 0.7 add_select_fusion.5
  263.8 2.3 add_select_fusion.4
  266.1 0.7 add_select_fusion.5
  266.8 2.3 add_select_fusion.4
  269.1 0.7 add_select_fusion.5
  269.8 2.3 add_select_fusion.4
  272.1 0.7 add_select_fusion.5
  272.9 2.3 add_select_fusion.4
  275.2 0.7 add_select_fusion.5
  275.9 3.5 select_reduce_fusion
  279.5 7.9 %fusion.6 = (f32[8,512]{1,0:T(8,128)S(1)}, f32[8,512]{1,0:T(8,128)S(1)}) fusion(f32[8,512,512]{2,1,0:T(8,128)} %get-tuple-element.157, f32[8,512]{1,0:T(8,128)S(1)} %maximum_maximum_fusion, pred[512,512]{0,1:T(8,128)(4,1)S(1)} %iota_compare_fusion.3, f32[8,512]{1,0:T(8,128)S(1)} %get-tuple-element.153, f32[8,512,512]{1,2,0:T(8,128)S(1)} %get-tuple-element.155, ...), kind=kLoop, calls=%fused_computation.21 | loop fusion | flops 18866176 | bytes 17108992 | tf_op jit(solution)/shard_map/vmap()/reduce_sum | solution.py:47
  287.4 2.2 bitcast_reduce_fusion
  289.6 3.3 fusion.8
  292.9 3.2 fusion.10
  296.1 9.2 %fusion.24 = bf16[512,8,128]{0,2,1:T(8,128)(2,1)} fusion(f32[8,512,128]{1,2,0:T(8,128)S(1)} %fusion.8, f32[8,512,128]{1,2,0:T(8,128)S(1)} %fusion.10, f32[512,8]{0,1:T(8,128)S(1)} %add_bitcast_fusion, f32[8,512,128]{2,1,0:T(8,128)S(1)} %get-tuple-element.116, f32[8,512,128]{2,1,0:T(8,128)} %collective-permute-done.3, ...), kind=kOutput, calls=%fused_computation.39 | convolution fusion | flops 3230138368 | bytes 17862656 | tf_op jit(solution)/shard_map/vmap()/dot_general | solution.py:55
  305.3 0.0 all-gather.5.cloned.1.call-update
  305.3 0.0 copy-start.1
  305.3 6.3 %copy.71 = bf16[2,1024,1024]{2,1,0:T(8,128)(2,1)} copy(bf16[2,1024,1024]{1,2,0:T(8,128)(2,1)} %bitcast.13) | data formatting | bytes 8388608 | tf_op jit(solution)/shard_map/all_to_all | solution.py:98
  311.6 31.1 %all-gather.5.cloned.1.call-done = bf16[512,2048]{0,1:T(8,128)(2,1)} async-done(((bf16[512,1024]{0,1:T(8,128)(2,1)}), bf16[512,2048]{0,1:T(8,128)(2,1)}) %all-gather.5.cloned.1.call-update) | async-done | bytes 2097168 | tf_op jit(solution)/shard_map/all_gather | solution.py:100
  342.8 6.1 %convolution_convert_fusion = bf16[512,1024]{1,0:T(8,128)(2,1)} fusion(bf16[512,2048]{0,1:T(8,128)(2,1)} %all-gather.5.cloned.1.call-done, bf16[2048,1024]{1,0:T(8,128)(2,1)} %bitcast.71), kind=kOutput, calls=%fused_computation.41 | convolution fusion | flops 2148007936 | bytes 7340032 | tf_op jit(solution)/shard_map/dot_general | solution.py:99
  (28 shorter events, 0.1 us)
Async XLA Ops:
  6.5 6.6 %copy-start = (bf16[8,512,128]{2,1,0:T(8,128)(2,1)S(1)}, bf16[8,512,128]{2,1,0:T(8,128)(2,1)}, u32[]{:S(2)}) copy-start(bf16[8,512,128]{2,1,0:T(8,128)(2,1)} %param.10) | copy-start | bytes 3145732
  6.5 6.5 %copy-start.3 = (s32[512,8]{0,1:T(8,128)S(1)}, s32[512,8]{0,1:T(8,128)}, u32[]{:S(2)}) copy-start(s32[512,8]{0,1:T(8,128)} %param.9) | copy-start | bytes 49156
  6.5 220.8 %all-gather.7.cloned.1.call-start = ((), (), s32[]{:S(2)}) async-start(), calls=%async_computation.2 | async-start | bytes 35651584 | tf_op jit(solution)/shard_map/all_gather | solution.py:17
  53.3 164.5 %collective-permute-start = (bf16[512,8,128]{2,0,1:T(8,128)(2,1)}, bf16[512,8,128]{2,0,1:T(8,128)(2,1)}, u32[]{:S(2)}, u32[]{:S(2)}) collective-permute-start(bf16[512,8,128]{2,0,1:T(8,128)(2,1)} %bitcast.4), channel_id=1, source_target_pairs={{0,2},{2,4},{4,6},{6,8},{8,10},{10,12},{12,14},{14,16},{16,18},{18... | collective-permute-start | bytes 3145736 | tf_op jit(solution)/shard_map/ppermute | solution.py:12
  56.6 236.2 %collective-permute-start.2 = (bf16[512,8,128]{0,2,1:T(8,128)(2,1)}, bf16[512,8,128]{0,2,1:T(8,128)(2,1)}, u32[]{:S(2)}, u32[]{:S(2)}) collective-permute-start(bf16[512,8,128]{0,2,1:T(8,128)(2,1)} %copy.66), channel_id=1, source_target_pairs={{0,2},{2,4},{4,6},{6,8},{8,10},{10,12},{12,14},{14,16},{16,18},{18... | collective-permute-start | bytes 3145736 | tf_op jit(solution)/shard_map/ppermute | solution.py:12
  61.2 234.9 %collective-permute-start.3 = (f32[8,512,128]{2,1,0:T(8,128)}, f32[8,512,128]{2,1,0:T(8,128)}, u32[]{:S(2)}, u32[]{:S(2)}) collective-permute-start(f32[8,512,128]{2,1,0:T(8,128)} %fusion.3), channel_id=1, source_target_pairs={{0,2},{2,4},{4,6},{6,8},{8,10},{10,12},{12,14},{14,16},{16,18},{18... | collective-permute-start | bytes 6291464 | tf_op jit(solution)/shard_map/ppermute | solution.py:12
  64.9 211.0 %collective-permute-start.1 = (f32[8,512]{1,0:T(8,128)S(1)}, f32[8,512]{1,0:T(8,128)S(1)}, u32[]{:S(2)}, u32[]{:S(2)}) collective-permute-start(f32[8,512]{1,0:T(8,128)S(1)} %convert_reduce_fusion), channel_id=1, source_target_pairs={{0,2},{2,4},{4,6},{6,8},{8,10},{10,12},{12,14},{14,16},{16,18},{18... | collective-permute-start | bytes 49160 | tf_op jit(solution)/shard_map/ppermute | solution.py:12
  73.2 232.1 %all-to-all-start = ((bf16[1024,2,1024]{0,2,1:T(8,128)(2,1)}), bf16[1024,2,1024]{0,2,1:T(8,128)(2,1)}, u32[]{:S(2)}, u32[]{:S(2)}) async-start(bf16[1024,2,1024]{0,2,1:T(8,128)(2,1)} %bitcast.70), calls=%async_computation | async-start | bytes 8388608 | tf_op jit(solution)/shard_map/all_to_all | solution.py:98
  78.8 263.9 %all-gather.5.cloned.1.call-start = ((), (), s32[]{:S(2)}) async-start(), calls=%async_computation.1 | async-start | bytes 3145728 | tf_op jit(solution)/shard_map/all_gather | solution.py:100
  78.9 138.8 %copy-start.2 = (bf16[512,8,128]{2,1,0:T(8,128)(2,1)S(1)}, bf16[512,8,128]{2,1,0:T(8,128)(2,1)}, u32[]{:S(2)}) copy-start(bf16[512,8,128]{2,1,0:T(8,128)(2,1)} %param.7) | copy-start | bytes 3145732
  275.9 11.5 %slice-start.2 = ((s8[8388608]{0:T(1024)(128)(4,1)}), s8[4194304]{0:T(1024)(128)(4,1)S(1)}, s32[]{:S(2)}) async-start(s8[8388608]{0:T(1024)(128)(4,1)} %bitcast.68), calls=%async_computation.5 | async-start | bytes 8388608
  275.9 13.7 %slice-start = ((s8[8388608]{0:T(1024)(128)(4,1)}), s8[4194304]{0:T(1024)(128)(4,1)S(1)}, s32[]{:S(2)}) async-start(s8[8388608]{0:T(1024)(128)(4,1)} %bitcast.66), calls=%async_computation.3 | async-start | bytes 8388608
  279.4 7.9 %slice-start.3 = ((s8[8388608]{0:T(1024)(128)(4,1)}), s8[4194304]{0:T(1024)(128)(4,1)S(1)}, s32[]{:S(2)}) async-start(s8[8388608]{0:T(1024)(128)(4,1)} %bitcast.68), calls=%async_computation.6 | async-start | bytes 8388608
  279.4 10.1 %slice-start.1 = ((s8[8388608]{0:T(1024)(128)(4,1)}), s8[4194304]{0:T(1024)(128)(4,1)S(1)}, s32[]{:S(2)}) async-start(s8[8388608]{0:T(1024)(128)(4,1)} %bitcast.66), calls=%async_computation.4 | async-start | bytes 8388608
  305.3 43.6 %copy-start.1 = (bf16[8,512,128]{2,1,0:T(8,128)(2,1)S(1)}, bf16[8,512,128]{2,1,0:T(8,128)(2,1)}, u32[]{:S(2)}) copy-start(bf16[8,512,128]{2,1,0:T(8,128)(2,1)} %param.10) | copy-start | bytes 3145732
Sparse Core Ops, SparseCore 0:
  13.2 214.1 all-gather.6
  305.4 37.2 all-gather.4
where the time goes:
time: 358 us; the launch traced here: 356 us
  blocking collectives  132 us (37%)
  other arithmetic  59.6 us (17%)
  local copies, waits for them, and re-layouts  55.6 us (16%)
  matrix products  41.2 us (12%)
  waiting for transfers between devices  35.1 us (10%)
  starting transfers between devices  18 us (5%)
  between operations  13.7 us (4%)
    all_gather x1, blocking collectives, prefix(): everything = jax.tree.map(lambda part: lax.all_gather(part, axis), x)  132 us
    select_n x32, other arithmetic, turn(): return jax.tree.map(lambda a, b: jnp.where(reached, a, b), new, before)  48.5 us
    gather x1, local copies, waits for them, and re-layouts, on_device(): book[index]  40.2 us
    all_gather x1, waiting for transfers between devices, on_device(): lax.all_gather(attended_all, 'head', axis=1, tiled=True)  31.1 us
    ppermute x4, starting transfers between devices, from_behind(): lax.ppermute(value, axis, [(source, source + steps) for source in range(f...  12.4 us
    dot_general x1, matrix products, attend(): jnp.dot(code_weight, cache_sum, precision=lax.Precision.HIGHEST)  9.17 us
    unnamed x20, local copies, waits for them, and re-layouts  9.13 us
    reduce_sum x1, other arithmetic, attend(): jnp.sum(cur_weight, axis=1) + jnp.sum(prev_weight, axis=1)  7.9 us
  transfers between devices with their start and end apart: 7, of which 2 were waited for; matrix products, arithmetic and copies ran while one was open for 40% of the time, Pallas kernels for 0%

commit v1 on v0

--- a/solution.py
+++ b/solution.py
@@ -4,6 +4,12 @@
 from jax.sharding import PartitionSpec as P
 
 BLOCK = 512
+
+
+def all_parts(value, axis, d):
+    parts = lax.all_gather(value, axis, axis=0, tiled=False)
+    full = jnp.concatenate(parts, axis=d)
+    return full
 
 
 def from_behind(value, axis, steps):
@@ -97,9 +103,7 @@
     attended_all = attended.reshape(tokens, local_heads * width)
     columns = lax.all_to_all(out_weight, "head", split_axis=1, concat_axis=0, tiled=True)
     summed = jnp.dot(
-        lax.all_gather(attended_all, "head", axis=1, tiled=True),
-        columns,
-        preferred_element_type=jnp.float32,
+        all_parts(attended_all, "head", 1), columns, preferred_element_type=jnp.float32
     )
     return summed.astype(jnp.bfloat16)
 

time: 358 us -> 358 us (level)
  waiting for transfers between devices: 35.1 us -> 41.4 us
  blocking collectives: 132 us -> 126 us
    all_gather x1, blocking collectives: 132 us -> 126 us  [prefix(): everything = jax.tree.map(lambda part: lax.all_gather(part, axis), x)]
    all_gather x1, waiting for transfers between devices: 31.1 us -> 37.4 us  [all_parts(): parts = lax.all_gather(value, axis, axis=0, tiled=False)]
where the time goes in v1:
time: 358 us; the launch traced here: 356 us
  blocking collectives  126 us (35%)
  other arithmetic  59.6 us (17%)
  local copies, waits for them, and re-layouts  56.9 us (16%)
  waiting for transfers between devices  41.4 us (12%)
  matrix products  40.4 us (11%)
  starting transfers between devices  18.2 us (5%)
  between operations  13.7 us (4%)
    all_gather x1, blocking collectives, prefix(): everything = jax.tree.map(lambda part: lax.all_gather(part, axis), x)  126 us
    select_n x32, other arithmetic, turn(): return jax.tree.map(lambda a, b: jnp.where(reached, a, b), new, before)  48.5 us
    gather x1, local copies, waits for them, and re-layouts, on_device(): book[index]  40.2 us
    all_gather x1, waiting for transfers between devices, all_parts(): parts = lax.all_gather(value, axis, axis=0, tiled=False)  37.4 us
    ppermute x4, starting transfers between devices, from_behind(): lax.ppermute(value, axis, [(source, source + steps) for source in range(f...  12.4 us
    unnamed x20, local copies, waits for them, and re-layouts  9.16 us
    dot_general x1, matrix products, attend(): jnp.dot(code_weight, cache_sum, precision=lax.Precision.HIGHEST)  8.39 us
    reduce_sum x1, other arithmetic, attend(): jnp.sum(cur_weight, axis=1) + jnp.sum(prev_weight, axis=1)  7.9 us
  transfers between devices with their start and end apart: 7, of which 2 were waited for; matrix products, arithmetic and copies ran while one was open for 40% of the time, Pallas kernels for 0%

profile of v1, /device:TPU:0, one launch (start us, length us, event | category | flops | bytes accessed | tf_op | source)
XLA Modules:
  0.0 356.3 jit_solution(2032987843232831951)
XLA Ops:
  6.5 2.5 copy.57
  9.0 4.0 %fusion.3 = f32[8,512,128]{2,1,0:T(8,128)} fusion(bf16[512,8,128]{0,2,1:T(8,128)(2,1)} %copy.57, s32[512,8]{0,1:T(8,128)} %param.9), kind=kOutput, calls=%fused_computation.18 | convolution fusion | flops 538968064 | bytes 3162112 | tf_op jit(solution)/shard_map/bths,bthd->bhsd/dot_general | solution.py:80
  13.0 0.0 all-gather.7.cloned.1.call-update
  13.1 40.2 %gather_fusion = bf16[4096,128]{1,0:T(8,128)(2,1)} fusion(bf16[8,512,128]{2,1,0:T(8,128)(2,1)S(1)} %copy-done, s32[4096]{0:T(1024)S(1)} %bitcast.73), kind=kCustom, calls=%fused_computation | custom fusion | bytes 2129920 | tf_op jit(solution)/shard_map/vmap()/gather | solution.py:73
  53.3 3.4 collective-permute-start
  56.6 4.5 %collective-permute-start.2 = (bf16[512,8,128]{0,2,1:T(8,128)(2,1)}, bf16[512,8,128]{0,2,1:T(8,128)(2,1)}, u32[]{:S(2)}, u32[]{:S(2)}) collective-permute-start(bf16[512,8,128]{0,2,1:T(8,128)(2,1)} %copy.57), channel_id=1, source_target_pairs={{0,2},{2,4},{4,6},{6,8},{8,10},{10,12},{12,14},{14,16},{16,18},{18... | collective-permute-start | bytes 3145736 | tf_op jit(solution)/shard_map/ppermute | solution.py:18
  61.2 2.6 collective-permute-start.3
  63.8 0.1 copy.54
  63.9 1.0 convert_reduce_fusion
  64.9 1.9 collective-permute-start.1
  66.8 6.5 %copy.62 = bf16[1024,2048]{0,1:T(8,128)(2,1)} copy(bf16[1024,2048]{1,0:T(8,128)(2,1)} %param.11) | data formatting | bytes 8388608 | tf_op args[4]
  73.3 6.2 %copy.63 = bf16[1024,2,1024]{2,0,1:T(8,128)(2,1)} copy(bf16[1024,2,1024]{0,2,1:T(8,128)(2,1)} %bitcast.78) | data formatting | bytes 8388608 | tf_op jit(solution)/shard_map/all_to_all | solution.py:104
  79.5 5.8 %all-to-all-start = ((bf16[1024,2,1024]{2,0,1:T(8,128)(2,1)}), bf16[1024,2,1024]{2,0,1:T(8,128)(2,1)}, u32[]{:S(2)}, u32[]{:S(2)}) async-start(bf16[1024,2,1024]{2,0,1:T(8,128)(2,1)} %copy.63), calls=%async_computation | async-start | bytes 8388608 | tf_op jit(solution)/shard_map/all_to_all | solution.py:104
  85.3 0.0 all-gather.5.cloned.1.call-start
  85.3 0.0 copy-start.2
  85.4 0.1 iota_compare_fusion.3
  85.4 126.1 %all-gather.1 = f32[128,512]{1,0:T(8,128)} all-gather(f32[8,512]{1,0:T(8,128)S(1)} %convert_reduce_fusion), channel_id=3, replica_groups=mesh['ctx'=16,'head'=2] {'ctx'}, dimensions={0}, use_global_device_ids=true | all-gather | bytes 278528 | tf_op jit(solution)/shard_map/all_gather | solution.py:23
  211.5 6.2 %fusion = (f32[8,512]{1,0:T(8,128)S(1)}, f32[8,512,512]{2,1,0:T(8,128)}) fusion(pred[512,512]{0,1:T(8,128)(4,1)S(1)} %iota_compare_fusion.3, bf16[8,512,128]{2,1,0:T(8,128)(2,1)} %bitcast.2, bf16[512,8,128]{2,1,0:T(8,128)(2,1)} %param.7), kind=kOutput, calls=%fused_computation.7 | convolution fusion | flops 543158272 | bytes 10764288 | tf_op jit(solution)/shard_map/vmap()/dot_general | solution.py:39
  217.7 5.7 %select_reduce_fusion.1 = (f32[8,512]{1,0:T(8,128)S(1)}, f32[8,512,512]{1,2,0:T(8,128)}) fusion(pred[]{:T(512)S(6)} %gt.6, bf16[512,8,128]{2,1,0:T(8,128)(2,1)S(1)} %copy-done.2, bf16[512,8,128]{2,0,1:T(8,128)(2,1)} %collective-permute-done), kind=kOutput, calls=%fused_computation.17 | convolution fusion | flops 543158272 | bytes 10502145 | tf_op jit(solution)/shard_map/vmap()/dot_general | solution.py:40
  223.4 3.9 %all-gather.7.cloned.1.call-done = f32[128,512,128]{2,1,0:T(8,128)} async-done(((f32[8,512,128]{2,1,0:T(8,128)}), f32[128,512,128]{2,1,0:T(8,128)}) %all-gather.7.cloned.1.call-update) | async-done | bytes 33554448 | tf_op jit(solution)/shard_map/all_gather | solution.py:23
  227.3 48.6 %while.16 = (s32[]{:T(128)}, f32[8,512,128]{2,1,0:T(8,128)S(1)}, f32[8,512]{1,0:T(8,128)S(1)}, s32[]{:T(128)}, f32[16,8,512,128]{3,2,1,0:T(8,128)}, /*index=5*/f32[16,8,512]{2,1,0:T(8,128)}, s32[]{:T(128)}, s32[]{:T(128)}) while((s32[]{:T(128)}, f32[8,512,128]{2,1,0:T(8,128)S(1)}, f32[8,512]{1,0:T(8,128)S(1)}, s32[]{:T(128)}, ...), condition=%wide.region_4.5_spmd.clone, body=%wide.region_3.4_spmd.clone.sunk | while | flops 1585156 | bytes 6340723 | solution.py:33
  227.3 2.3 add_select_fusion.4
  229.6 0.7 add_select_fusion.5
  230.4 2.3 add_select_fusion.4
  232.7 0.7 add_select_fusion.5
  233.4 2.3 add_select_fusion.4
  235.7 0.7 add_select_fusion.5
  236.4 2.3 add_select_fusion.4
  238.8 0.7 add_select_fusion.5
  239.5 2.3 add_select_fusion.4
  241.8 0.7 add_select_fusion.5
  242.5 2.3 add_select_fusion.4
  244.8 0.7 add_select_fusion.5
  245.5 2.3 add_select_fusion.4
  247.9 0.7 add_select_fusion.5
  248.6 2.3 add_select_fusion.4
  250.9 0.7 add_select_fusion.5
  251.6 2.3 add_select_fusion.4
  253.9 0.7 add_select_fusion.5
  254.7 2.3 add_select_fusion.4
  257.0 0.7 add_select_fusion.5
  257.7 2.3 add_select_fusion.4
  260.0 0.7 add_select_fusion.5
  260.7 2.3 add_select_fusion.4
  263.0 0.7 add_select_fusion.5
  263.8 2.3 add_select_fusion.4
  266.1 0.7 add_select_fusion.5
  266.8 2.3 add_select_fusion.4
  269.1 0.7 add_select_fusion.5
  269.8 2.3 add_select_fusion.4
  272.1 0.7 add_select_fusion.5
  272.9 2.3 add_select_fusion.4
  275.2 0.7 add_select_fusion.5
  275.9 3.5 select_reduce_fusion
  279.5 7.9 %fusion.6 = (f32[8,512]{1,0:T(8,128)S(1)}, f32[8,512]{1,0:T(8,128)S(1)}) fusion(f32[8,512,512]{2,1,0:T(8,128)} %get-tuple-element.157, f32[8,512]{1,0:T(8,128)S(1)} %maximum_maximum_fusion, pred[512,512]{0,1:T(8,128)(4,1)S(1)} %iota_compare_fusion.3, f32[8,512]{1,0:T(8,128)S(1)} %get-tuple-element.153, f32[8,512,512]{1,2,0:T(8,128)S(1)} %get-tuple-element.155, ...), kind=kLoop, calls=%fused_computation.21 | loop fusion | flops 18866176 | bytes 17108992 | tf_op jit(solution)/shard_map/vmap()/reduce_sum | solution.py:53
  287.4 2.2 bitcast_reduce_fusion
  289.6 3.3 fusion.8
  292.9 3.2 fusion.10
  296.1 8.4 %fusion.27 = bf16[512,8,128]{0,2,1:T(8,128)(2,1)S(1)} fusion(f32[8,512,128]{1,2,0:T(8,128)S(1)} %fusion.8, f32[8,512,128]{1,2,0:T(8,128)S(1)} %fusion.10, f32[512,8]{0,1:T(8,128)S(1)} %add_bitcast_fusion, f32[8,512,128]{2,1,0:T(8,128)S(1)} %get-tuple-element.116, f32[8,512,128]{2,1,0:T(8,128)} %collective-permute-done.3, ...), kind=kOutput, calls=%fused_computation.43 | convolution fusion | flops 3230138368 | bytes 17862656 | tf_op jit(solution)/shard_map/vmap()/dot_general | solution.py:61
  304.5 1.3 copy.61
  305.8 0.0 all-gather.5.cloned.1.call-update
  305.9 0.0 copy-start.1
  305.9 37.4 %all-gather.5.cloned.1.call-done = bf16[2,512,1024]{2,1,0:T(8,128)(2,1)} async-done(((bf16[1,512,1024]{2,1,0:T(8,128)(2,1)}), bf16[2,512,1024]{2,1,0:T(8,128)(2,1)}) %all-gather.5.cloned.1.call-update) | async-done | bytes 2097168 | tf_op jit(solution)/shard_map/all_gather | solution.py:10
  343.3 6.1 %bitcast_convert_fusion.2 = bf16[512,1024]{1,0:T(8,128)(2,1)} fusion(bf16[1024,2,1024]{2,0,1:T(8,128)(2,1)} %all-to-all-done, bf16[2,512,1024]{2,1,0:T(8,128)(2,1)} %all-gather.5.cloned.1.call-done), kind=kOutput, calls=%fused_computation.40 | convolution fusion | flops 2148007936 | bytes 7340032 | tf_op jit(solution)/shard_map/dot_general | solution.py:105
  (29 shorter events, 0.1 us)
Async XLA Ops:
  6.5 6.6 %copy-start = (bf16[8,512,128]{2,1,0:T(8,128)(2,1)S(1)}, bf16[8,512,128]{2,1,0:T(8,128)(2,1)}, u32[]{:S(2)}) copy-start(bf16[8,512,128]{2,1,0:T(8,128)(2,1)} %param.10) | copy-start | bytes 3145732
  6.5 6.5 %copy-start.3 = (s32[512,8]{0,1:T(8,128)S(1)}, s32[512,8]{0,1:T(8,128)}, u32[]{:S(2)}) copy-start(s32[512,8]{0,1:T(8,128)} %param.9) | copy-start | bytes 49156
  6.5 220.8 %all-gather.7.cloned.1.call-start = ((), (), s32[]{:S(2)}) async-start(), calls=%async_computation.2 | async-start | bytes 35651584 | tf_op jit(solution)/shard_map/all_gather | solution.py:23
  53.3 164.5 %collective-permute-start = (bf16[512,8,128]{2,0,1:T(8,128)(2,1)}, bf16[512,8,128]{2,0,1:T(8,128)(2,1)}, u32[]{:S(2)}, u32[]{:S(2)}) collective-permute-start(bf16[512,8,128]{2,0,1:T(8,128)(2,1)} %bitcast.4), channel_id=1, source_target_pairs={{0,2},{2,4},{4,6},{6,8},{8,10},{10,12},{12,14},{14,16},{16,18},{18... | collective-permute-start | bytes 3145736 | tf_op jit(solution)/shard_map/ppermute | solution.py:18
  56.6 236.2 %collective-permute-start.2 = (bf16[512,8,128]{0,2,1:T(8,128)(2,1)}, bf16[512,8,128]{0,2,1:T(8,128)(2,1)}, u32[]{:S(2)}, u32[]{:S(2)}) collective-permute-start(bf16[512,8,128]{0,2,1:T(8,128)(2,1)} %copy.57), channel_id=1, source_target_pairs={{0,2},{2,4},{4,6},{6,8},{8,10},{10,12},{12,14},{14,16},{16,18},{18... | collective-permute-start | bytes 3145736 | tf_op jit(solution)/shard_map/ppermute | solution.py:18
  61.2 234.9 %collective-permute-start.3 = (f32[8,512,128]{2,1,0:T(8,128)}, f32[8,512,128]{2,1,0:T(8,128)}, u32[]{:S(2)}, u32[]{:S(2)}) collective-permute-start(f32[8,512,128]{2,1,0:T(8,128)} %fusion.3), channel_id=1, source_target_pairs={{0,2},{2,4},{4,6},{6,8},{8,10},{10,12},{12,14},{14,16},{16,18},{18... | collective-permute-start | bytes 6291464 | tf_op jit(solution)/shard_map/ppermute | solution.py:18
  64.9 211.0 %collective-permute-start.1 = (f32[8,512]{1,0:T(8,128)S(1)}, f32[8,512]{1,0:T(8,128)S(1)}, u32[]{:S(2)}, u32[]{:S(2)}) collective-permute-start(f32[8,512]{1,0:T(8,128)S(1)} %convert_reduce_fusion), channel_id=1, source_target_pairs={{0,2},{2,4},{4,6},{6,8},{8,10},{10,12},{12,14},{14,16},{16,18},{18... | collective-permute-start | bytes 49160 | tf_op jit(solution)/shard_map/ppermute | solution.py:18
  79.5 226.4 %all-to-all-start = ((bf16[1024,2,1024]{2,0,1:T(8,128)(2,1)}), bf16[1024,2,1024]{2,0,1:T(8,128)(2,1)}, u32[]{:S(2)}, u32[]{:S(2)}) async-start(bf16[1024,2,1024]{2,0,1:T(8,128)(2,1)} %copy.63), calls=%async_computation | async-start | bytes 8388608 | tf_op jit(solution)/shard_map/all_to_all | solution.py:104
  85.3 258.0 %all-gather.5.cloned.1.call-start = ((), (), s32[]{:S(2)}) async-start(), calls=%async_computation.1 | async-start | bytes 3145728 | tf_op jit(solution)/shard_map/all_gather | solution.py:10
  85.3 132.4 %copy-start.2 = (bf16[512,8,128]{2,1,0:T(8,128)(2,1)S(1)}, bf16[512,8,128]{2,1,0:T(8,128)(2,1)}, u32[]{:S(2)}) copy-start(bf16[512,8,128]{2,1,0:T(8,128)(2,1)} %param.7) | copy-start | bytes 3145732
  275.9 11.5 %slice-start.2 = ((s8[8388608]{0:T(1024)(128)(4,1)}), s8[4194304]{0:T(1024)(128)(4,1)S(1)}, s32[]{:S(2)}) async-start(s8[8388608]{0:T(1024)(128)(4,1)} %bitcast.76), calls=%async_computation.5 | async-start | bytes 8388608
  275.9 13.7 %slice-start = ((s8[8388608]{0:T(1024)(128)(4,1)}), s8[4194304]{0:T(1024)(128)(4,1)S(1)}, s32[]{:S(2)}) async-start(s8[8388608]{0:T(1024)(128)(4,1)} %bitcast.74), calls=%async_computation.3 | async-start | bytes 8388608
  279.4 7.9 %slice-start.3 = ((s8[8388608]{0:T(1024)(128)(4,1)}), s8[4194304]{0:T(1024)(128)(4,1)S(1)}, s32[]{:S(2)}) async-start(s8[8388608]{0:T(1024)(128)(4,1)} %bitcast.76), calls=%async_computation.6 | async-start | bytes 8388608
  279.4 10.1 %slice-start.1 = ((s8[8388608]{0:T(1024)(128)(4,1)}), s8[4194304]{0:T(1024)(128)(4,1)S(1)}, s32[]{:S(2)}) async-start(s8[8388608]{0:T(1024)(128)(4,1)} %bitcast.74), calls=%async_computation.4 | async-start | bytes 8388608
  305.9 43.6 %copy-start.1 = (bf16[8,512,128]{2,1,0:T(8,128)(2,1)S(1)}, bf16[8,512,128]{2,1,0:T(8,128)(2,1)}, u32[]{:S(2)}) copy-start(bf16[8,512,128]{2,1,0:T(8,128)(2,1)} %param.10) | copy-start | bytes 3145732
Sparse Core Ops, SparseCore 0:
  13.2 214.1 all-gather.6
  306.0 37.2 all-gather.4
